TPU v7x, 32 devices: a whole 2x2x4 slice. The times are simulated.
32 devices in a mesh: row: 4 (over y, x), col: 8 (over z, core).
Axes of the slice: x: 2, y: 2, z: 4, core: 2. Of those that a mesh axis runs over, the one named last changes fastest.
Arguments:
- panel: float32 [12288, 512], P(('row', 'col')), may hold values from -0.054126588 to 0.054126588
- trailing: float32 [12288, 4096], P('row', 'col'), may hold values from -6 to 6
- counts: int32 [4], P('row'), may hold values from 1 to 6, 14 in all
Outputs:
- upper: float32 [512, 512], replicated
- projected: float32 [512, 4096], P(None, 'col')
Inputs may be any that keep to these rules, and one draw needn't show every extreme that they name: `counts`: the valid tiles of a block are its first ones; some grid row has all 6 valid.
All inputs are finite; a program needn't handle non-finite values.
Results may differ from a plain program's by a relative error of at most 0.0003.
Values sent between devices are 32-bit elements; how exact they have to be, the bound alone decides.
A program may use at most 64 MiB of HBM per device.

v0:
```python
import functools

import jax
import jax.numpy as jnp
from jax import lax
from jax.experimental import pallas as pl
from jax.experimental.pallas import tpu as pltpu
from jax.sharding import PartitionSpec as P

MESH = pl.DeviceIdType.MESH
LANES = 128
GROUP = 8


def split(x):
    high = x.astype(jnp.bfloat16)
    return high, (x - high.astype(jnp.float32)).astype(jnp.bfloat16)


def dot3(left, right, dims):
    one = functools.partial(
        lax.dot_general, dimension_numbers=(dims, ((), ())), preferred_element_type=jnp.float32
    )
    return one(left[0], right[0]) + (one(left[0], right[1]) + one(left[1], right[0]))


def bits_of(axis, size):
    return [(axis, 1 << b) for b in range(size.bit_length() - 1)]


def plan(rows, order):
    steps = []
    for axis, bit in order:
        halve = rows % (2 * GROUP) == 0
        steps.append((axis, bit, rows, halve))
        rows = rows // 2 if halve else rows
    return steps


def partner(axis, bit):
    me = lax.axis_index(axis)
    mine = lax.rem(me // bit, 2)
    return mine, {axis: me + bit - 2 * bit * mine}


def greet(axis_bits):
    barrier = pltpu.get_barrier_semaphore()
    for axis, bit in axis_bits:
        _, other = partner(axis, bit)
        pl.semaphore_signal(barrier, inc=1, device_id=other, device_id_type=MESH)
    pl.semaphore_wait(barrier, len(axis_bits))


def reduce_all(acc, out, landing, send, recv, streams):
    count = len(streams[0][1])
    offsets = [[start] for start, _ in streams]

    def copy(n, src, dst, other):
        return pltpu.make_async_remote_copy(
            src_ref=src, dst_ref=dst, send_sem=send.at[n], recv_sem=recv.at[n],
            device_id=other, device_id_type=MESH,
        )

    pending = []
    slot = 0
    for s in range(count):
        copies = []
        for i, (_, steps) in enumerate(streams):
            axis, bit, rows, halve = steps[s]
            mine, other = partner(axis, bit)
            at = offsets[i][-1]
            size = rows // 2 if halve else rows
            keep = at + mine * size if halve else at
            away = at + (1 - mine) * size if halve else at
            keep, away = pl.multiple_of(keep, GROUP), pl.multiple_of(away, GROUP)
            land = landing.at[pl.ds(slot, size)]
            c = copy(2 * len(streams) * s + i, acc.at[pl.ds(away, size)], land, other)
            c.start()
            copies.append((c, keep, size, slot, halve))
            offsets[i].append(keep)
            slot += size
        for c, keep, size, here, halve in copies:
            if halve:
                c.wait_recv()
                pending.append(c)
            else:
                c.wait()
            target = out if s == count - 1 else acc
            target[pl.ds(keep, size)] = acc[pl.ds(keep, size)] + landing[pl.ds(here, size)]
    for c in pending:
        c.wait_send()
    pending = []
    for s in reversed(range(count)):
        copies = []
        for i, (_, steps) in enumerate(streams):
            axis, bit, rows, halve = steps[s]
            if not halve:
                continue
            _, other = partner(axis, bit)
            size = rows // 2
            region = out.at[pl.ds(offsets[i][s + 1], size)]
            c = copy(2 * len(streams) * s + len(streams) + i, region, region, other)
            c.start()
            copies.append(c)
        for c in copies:
            c.wait_recv()
        pending += copies
    for c in pending:
        c.wait_send()


def landing_rows(streams):
    return sum(r // 2 if h else r for _, steps in streams for _, _, r, h in steps)


def blocks_of(width):
    tiles = width // LANES
    return [(i, j) for i in range(tiles) for j in range(i, tiles)]


def gram_kernel(streams, order, piece_ref, out_ref, acc, landing, send, recv):
    high, low = split(piece_ref[...])
    for n, (i, j) in enumerate(blocks_of(piece_ref.shape[1])):
        a, b = slice(i * LANES, (i + 1) * LANES), slice(j * LANES, (j + 1) * LANES)
        acc[n * LANES:(n + 1) * LANES] = dot3(
            (high[:, a], low[:, a]), (high[:, b], low[:, b]), ((0,), (0,))
        )
    greet(order)
    reduce_all(acc, out_ref, landing, send, recv, streams)


def sum_kernel(streams, order, in_ref, out_ref, acc, landing, send, recv):
    acc[...] = in_ref[...]
    greet(order)
    reduce_all(acc, out_ref, landing, send, recv, streams)


def two_streams(rows, first, second):
    half = rows // 2
    return [(0, plan(half, first)), (half, plan(half, second))]


def call_reducing(kernel, value, rows, lanes, streams, order, ident):
    copies = 2 * len(streams) * len(streams[0][1])
    return pl.pallas_call(
        functools.partial(kernel, streams, order),
        out_shape=jax.ShapeDtypeStruct((rows, lanes), jnp.float32),
        in_specs=[pl.BlockSpec(memory_space=pltpu.VMEM)],
        out_specs=pl.BlockSpec(memory_space=pltpu.VMEM),
        scratch_shapes=[
            pltpu.VMEM((rows, lanes), jnp.float32),
            pltpu.VMEM((landing_rows(streams), lanes), jnp.float32),
            pltpu.SemaphoreType.DMA((copies,)),
            pltpu.SemaphoreType.DMA((copies,)),
        ],
        compiler_params=pltpu.CompilerParams(collective_id=ident, has_side_effects=True),
        cost_estimate=pl.CostEstimate(flops=10**9, bytes_accessed=2 * 10**7, transcendentals=0),
    )(value)


def factor_group(work, g):
    at = g * GROUP
    left = work[at:at + GROUP, :LANES]
    right = work[at:at + GROUP, LANES:]
    rows = lax.broadcasted_iota(jnp.int32, (GROUP, LANES), 0)
    columns = [
        jnp.broadcast_to(left[:, at + j:at + j + 1], (GROUP, LANES)) for j in range(GROUP)
    ]
    for j in range(GROUP):
        scale = lax.rsqrt(columns[j][j:j + 1, :])
        factor = columns[j] * scale
        below = jnp.where(rows > j, factor, 0.0)
        left_j, right_j = left[j:j + 1, :] * scale, right[j:j + 1, :] * scale
        left = jnp.where(rows == j, left_j, left - below * left_j)
        right = jnp.where(rows == j, right_j, right - below * right_j)
        for k in range(j + 1, GROUP):
            columns[k] = columns[k] - below * factor[k:k + 1, :]
    work[at:at + GROUP, :LANES] = left
    work[at:at + GROUP, LANES:] = right
    rest = LANES - at - GROUP
    if rest:
        high, low = split(jnp.concatenate([left, right], axis=1))
        shift = (high[:, at + GROUP:LANES], low[:, at + GROUP:LANES])
        work[at + GROUP:] = work[at + GROUP:] - dot3(shift, (high, low), ((0,), (0,)))


def factor_kernel(packed_ref, upper_ref, inverse_ref, whole, work):
    width = upper_ref.shape[0]
    whole[...] = jnp.zeros_like(whole)
    for n, (i, j) in enumerate(blocks_of(width)):
        whole[i * LANES:(i + 1) * LANES, j * LANES:(j + 1) * LANES] = packed_ref[
            n * LANES:(n + 1) * LANES
        ]
    square = lax.broadcasted_iota(jnp.int32, (LANES, LANES), 0)
    across = lax.broadcasted_iota(jnp.int32, (LANES, LANES), 1)
    unit = (square == across).astype(jnp.float32)
    for t in range(width // LANES):
        a, b = t * LANES, (t + 1) * LANES
        whole[a:b, width + a:width + b] = unit

    for t in range(width // LANES):
        a, b = t * LANES, (t + 1) * LANES
        work[:, :LANES] = whole[a:b, a:b]
        work[:, LANES:] = unit
        for g in range(LANES // GROUP):
            factor_group(work, g)
        inverse = split(work[:, LANES:])
        row = dot3(inverse, split(whole[a:b, a:width + b]), ((1,), (0,)))
        whole[a:b, a:width + b] = row
        whole[a:b, a:b] = jnp.where(across >= square, work[:, :LANES], 0.0)
        if t:
            whole[a:b, :a] = jnp.zeros((LANES, a), jnp.float32)
        if b < width:
            high, low = split(row)
            rest = width - b
            shift = (high[:, LANES:LANES + rest], low[:, LANES:LANES + rest])
            tail = (high[:, LANES:], low[:, LANES:])
            whole[b:, b:width + b] = whole[b:, b:width + b] - dot3(shift, tail, ((0,), (0,)))
    upper_ref[...] = whole[:, :width]
    inverse_ref[...] = whole[:, width:]


def factorize(packed, width):
    square = jax.ShapeDtypeStruct((width, width), jnp.float32)
    return pl.pallas_call(
        factor_kernel,
        out_shape=(square, square),
        in_specs=[pl.BlockSpec(memory_space=pltpu.VMEM)],
        out_specs=[pl.BlockSpec(memory_space=pltpu.VMEM)] * 2,
        scratch_shapes=[
            pltpu.VMEM((width, 2 * width), jnp.float32),
            pltpu.VMEM((LANES, 2 * LANES), jnp.float32),
        ],
        cost_estimate=pl.CostEstimate(flops=10**9, bytes_accessed=10**8, transcendentals=0),
    )(packed)


def body(n_row, n_col, panel, trailing, counts):
    width = panel.shape[1]
    valid = counts[0]
    piece = lax.all_gather(panel, "col", axis=0, tiled=True)

    own = lax.axis_index("col") * panel.shape[0] + lax.iota(jnp.int32, panel.shape[0])
    masked = jnp.where((own // width < valid)[:, None], panel, 0.0)
    rows, columns = bits_of("row", n_row), bits_of("col", n_col)
    turned = rows[len(rows) // 2:] + rows[:len(rows) // 2]
    order = columns[:1] + rows + columns[1:]
    packed_rows = len(blocks_of(width)) * LANES
    packed = call_reducing(
        gram_kernel, masked, packed_rows, LANES,
        two_streams(packed_rows, order, columns[:1] + turned + columns[1:]), order, 0,
    )
    upper, inverse = factorize(packed, width)

    indices = lax.iota(jnp.int32, piece.shape[0])
    piece = jnp.where((indices // width < valid)[:, None], piece, 0.0)
    cross = lax.dot_general(
        piece, trailing, (((0,), (0,)), ((), ())),
        precision=lax.Precision.HIGH, preferred_element_type=jnp.float32,
    )
    cross = call_reducing(
        sum_kernel, cross, width, cross.shape[1], two_streams(width, rows, turned), rows, 1
    )
    projected = lax.dot(
        inverse, cross, precision=lax.Precision.HIGH, preferred_element_type=jnp.float32
    )
    return (upper, projected)


def solution(mesh):
    return jax.shard_map(
        functools.partial(body, mesh.shape["row"], mesh.shape["col"]),
        mesh=mesh,
        in_specs=(P(("row", "col"), None), P("row", "col"), P("row")),
        out_specs=(P(), P(None, "col")),
        check_vma=False,
    )
```

profile of v0, /device:TPU:0, one launch (start us, length us, event | category | flops | bytes accessed | tf_op | source)
XLA Modules:
  0.0 129.4 jit_solution(9098773451873302151)
XLA Ops:
  7.2 0.0 all-gather.2.cloned.1.call-start
  7.2 0.7 all-gather.2.cloned.1.call-update
  8.6 2.1 %broadcast_select_fusion.piece_ref = f32[384,512]{1,0:T(8,128)} fusion(f32[384,512]{1,0:T(8,128)} %param.3, pred[384]{0:T(512)(128)(4,1)S(1)} %fusion.9), kind=kLoop, calls=%fused_computation.4 | loop fusion | flops 196608 | bytes 1573248 | tf_op jit(solution)/shard_map/jit(_where)/select_n | solution.py:244
  10.7 40.9 %shard_map.50.packed_ref = f32[1280,128]{1,0:T(8,128)} custom-call(f32[384,512]{1,0:T(8,128)} %broadcast_select_fusion.piece_ref), custom_call_target="tpu_custom_call" | custom-call | flops 1000000000 | bytes 20000000 | tf_op jit(solution)/shard_map/pallas_call | solution.py:145
  51.6 31.2 %shard_map.51 = (f32[512,512]{1,0:T(8,128)}, f32[512,512]{1,0:T(8,128)}) custom-call(f32[1280,128]{1,0:T(8,128)} %shard_map.50.packed_ref), custom_call_target="tpu_custom_call" | custom-call | flops 1000000000 | bytes 100000000 | tf_op jit(solution)/shard_map/pallas_call | solution.py:225
  82.8 0.0 copy-start
  82.8 0.0 all-gather.2.cloned.1.call-done
  82.8 11.5 %fusion.in_ref = f32[512,512]{1,0:T(8,128)} fusion(f32[3072,512]{1,0:T(8,128)} %param.4, f32[3072,512]{1,0:T(8,128)} %all-gather.2.cloned.1.call-done, pred[3072]{0:T(1024)(128)(4,1)S(1)} %fusion.4), kind=kOutput, calls=%fused_computation | convolution fusion | flops 4833411072 | bytes 13634560 | tf_op jit(solution)/shard_map/dot_general | solution.py:257
  94.3 25.0 %shard_map.52 = f32[512,512]{1,0:T(8,128)} custom-call(f32[512,512]{1,0:T(8,128)} %fusion.in_ref), custom_call_target="tpu_custom_call" | custom-call | flops 1000000000 | bytes 20000000 | tf_op jit(solution)/shard_map/pallas_call | solution.py:145
  119.3 0.0 copy-done
  119.3 3.2 %fusion.13 = f32[512,512]{1,0:T(8,128)} fusion(f32[512,512]{1,0:T(8,128)S(1)} %copy-done, f32[512,512]{1,0:T(8,128)} %shard_map.52), kind=kOutput, calls=%fused_computation.24 | convolution fusion | flops 805306368 | bytes 3145728 | tf_op jit(solution)/shard_map/dot_general | solution.py:264
  (2 shorter events, 0.0 us)
Async XLA Ops:
  7.2 75.6 %all-gather.2.cloned.1.call-start = ((), (), s32[]{:S(2)}) async-start(), calls=%async_computation | async-start | bytes 7077888 | tf_op jit(solution)/shard_map/all_gather | solution.py:241
  82.8 36.6 %copy-start = (f32[512,512]{1,0:T(8,128)S(1)}, f32[512,512]{1,0:T(8,128)}, u32[]{:S(2)}) copy-start(f32[512,512]{1,0:T(8,128)} %get-tuple-element.5) | copy-start | bytes 3145732
Sparse Core Ops, SparseCore 0:
  9.6 69.0 all-gather.1
where the time goes:
time: 130 us; the launch traced here: 129 us
  Pallas kernels  97 us (75%)
  matrix products  14.7 us (11%)
  between operations  14.7 us (11%)
  other arithmetic  2.16 us (2%)
    pallas_call x2, Pallas kernels, call_reducing(): pl.pallas_call(functools.partial(kernel, streams, order), out_shape=jax.S...  65.9 us
    pallas_call x1, Pallas kernels, factorize(): pl.pallas_call(factor_kernel, out_shape=(square, square), in_specs=[pl.Bl...  31.2 us
    dot_general x1, matrix products, body(): lax.dot_general(piece, trailing, (((0,), (0,)), ((), ())), precision=lax....  11.5 us
    dot_general x1, matrix products, body(): lax.dot(inverse, cross, precision=lax.Precision.HIGH, preferred_element_t...  3.2 us
  transfers between devices with their start and end apart: 1, of which 0 were waited for; matrix products, arithmetic and copies ran while one was open for 2% of the time, Pallas kernels for 56%

commit v1 on v0

--- a/solution.py
+++ b/solution.py
@@ -10,6 +10,8 @@
 MESH = pl.DeviceIdType.MESH
 LANES = 128
 GROUP = 8
+CORES = 2
+HALVES = 2
 
 
 def split(x):
@@ -43,15 +45,11 @@
     return mine, {axis: me + bit - 2 * bit * mine}
 
 
-def greet(axis_bits):
-    barrier = pltpu.get_barrier_semaphore()
-    for axis, bit in axis_bits:
-        _, other = partner(axis, bit)
-        pl.semaphore_signal(barrier, inc=1, device_id=other, device_id_type=MESH)
-    pl.semaphore_wait(barrier, len(axis_bits))
-
-
-def reduce_all(acc, out, landing, send, recv, streams):
+def nothing():
+    pass
+
+
+def reduce_all(acc, out, landing, send, recv, streams, hooks={}):
     count = len(streams[0][1])
     offsets = [[start] for start, _ in streams]
 
@@ -79,6 +77,7 @@
             copies.append((c, keep, size, slot, halve))
             offsets[i].append(keep)
             slot += size
+        hooks.get(("fold", s), nothing)()
         for c, keep, size, here, halve in copies:
             if halve:
                 c.wait_recv()
@@ -102,6 +101,7 @@
             c = copy(2 * len(streams) * s + len(streams) + i, region, region, other)
             c.start()
             copies.append(c)
+        hooks.get(("spread", s), nothing)()
         for c in copies:
             c.wait_recv()
         pending += copies
@@ -118,44 +118,9 @@
     return [(i, j) for i in range(tiles) for j in range(i, tiles)]
 
 
-def gram_kernel(streams, order, piece_ref, out_ref, acc, landing, send, recv):
-    high, low = split(piece_ref[...])
-    for n, (i, j) in enumerate(blocks_of(piece_ref.shape[1])):
-        a, b = slice(i * LANES, (i + 1) * LANES), slice(j * LANES, (j + 1) * LANES)
-        acc[n * LANES:(n + 1) * LANES] = dot3(
-            (high[:, a], low[:, a]), (high[:, b], low[:, b]), ((0,), (0,))
-        )
-    greet(order)
-    reduce_all(acc, out_ref, landing, send, recv, streams)
-
-
-def sum_kernel(streams, order, in_ref, out_ref, acc, landing, send, recv):
-    acc[...] = in_ref[...]
-    greet(order)
-    reduce_all(acc, out_ref, landing, send, recv, streams)
-
-
 def two_streams(rows, first, second):
     half = rows // 2
     return [(0, plan(half, first)), (half, plan(half, second))]
-
-
-def call_reducing(kernel, value, rows, lanes, streams, order, ident):
-    copies = 2 * len(streams) * len(streams[0][1])
-    return pl.pallas_call(
-        functools.partial(kernel, streams, order),
-        out_shape=jax.ShapeDtypeStruct((rows, lanes), jnp.float32),
-        in_specs=[pl.BlockSpec(memory_space=pltpu.VMEM)],
-        out_specs=pl.BlockSpec(memory_space=pltpu.VMEM),
-        scratch_shapes=[
-            pltpu.VMEM((rows, lanes), jnp.float32),
-            pltpu.VMEM((landing_rows(streams), lanes), jnp.float32),
-            pltpu.SemaphoreType.DMA((copies,)),
-            pltpu.SemaphoreType.DMA((copies,)),
-        ],
-        compiler_params=pltpu.CompilerParams(collective_id=ident, has_side_effects=True),
-        cost_estimate=pl.CostEstimate(flops=10**9, bytes_accessed=2 * 10**7, transcendentals=0),
-    )(value)
 
 
 def factor_group(work, g):
@@ -184,11 +149,153 @@
         work[at + GROUP:] = work[at + GROUP:] - dot3(shift, (high, low), ((0,), (0,)))
 
 
-def factor_kernel(packed_ref, upper_ref, inverse_ref, whole, work):
-    width = upper_ref.shape[0]
+def kernel(
+    n_row, n_col, counts_ref, panel_ref, trailing_hbm, upper_ref, out_ref,
+    pack, packed, pack_land, send, recv, gathered, trailing, total, summed, land, send2, recv2,
+    whole, work, load, right_s, left_s, mate_s, line_r, mate_r,
+):
+    width = panel_ref.shape[1]
+    rows_dev = panel_ref.shape[0]
+    half = rows_dev // HALVES
+    lines = n_col // CORES
+    col = lax.axis_index("col")
+    z, core = col // CORES, lax.rem(col, CORES)
+    row_bits, col_bits = bits_of("row", n_row), bits_of("col", n_col)
+    turned = row_bits[len(row_bits) // 2:] + row_bits[:len(row_bits) // 2]
+    order = col_bits[:1] + row_bits + col_bits[1:]
+    other_order = col_bits[:1] + turned + col_bits[1:]
+    fold_streams = two_streams(packed.shape[0], order, other_order)
+    sum_streams = two_streams(width, row_bits, turned)
+
+    fetch = pltpu.make_async_copy(trailing_hbm, trailing, load)
+    fetch.start()
+
+    def place(src, h):
+        at = (src * CORES + core) * rows_dev + h * half
+        return gathered.at[pl.ds(pl.multiple_of(at, GROUP), half)]
+
+    def send_copy(src, h, origin, sems, to):
+        return pltpu.make_async_remote_copy(
+            src_ref=origin, dst_ref=place(src, h), send_sem=sems.at[src * HALVES + h],
+            recv_sem=line_r.at[src * HALVES + h], device_id={"col": to}, device_id_type=MESH,
+        )
+
+    def mate_copy(src, h, origin):
+        return pltpu.make_async_remote_copy(
+            src_ref=origin, dst_ref=place(src, h), send_sem=mate_s.at[src * HALVES + h],
+            recv_sem=mate_r.at[src * HALVES + h], device_id={"col": col + 1 - 2 * core},
+            device_id_type=MESH,
+        )
+
+    def start_own(h):
+        origin = panel_ref.at[pl.ds(h * half, half)]
+
+        @pl.when(z < lines - 1)
+        def _():
+            send_copy(z, h, origin, right_s, col + CORES).start()
+
+        @pl.when(z > 0)
+        def _():
+            send_copy(z, h, origin, left_s, col - CORES).start()
+
+        mate_copy(z, h, origin).start()
+
+    def relay(s, h):
+        @pl.when(z >= s)
+        def _():
+            src = z - s
+            send_copy(src, h, place(src, h), right_s, col).wait_recv()
+
+            @pl.when(z < lines - 1)
+            def _():
+                send_copy(src, h, place(src, h), right_s, col + CORES).start()
+
+            mate_copy(src, h, place(src, h)).start()
+
+        @pl.when(z + s < lines)
+        def _():
+            src = z + s
+            send_copy(src, h, place(src, h), left_s, col).wait_recv()
+
+            @pl.when(z > 0)
+            def _():
+                send_copy(src, h, place(src, h), left_s, col - CORES).start()
+
+            mate_copy(src, h, place(src, h)).start()
+
+    limit = counts_ref[0] * width
+
+    def multiply(src):
+        rows = CORES * rows_dev
+        at = pl.multiple_of(src * rows, GROUP)
+        index = at + lax.broadcasted_iota(jnp.int32, (rows, LANES), 0)
+        right = split(trailing[pl.ds(at, rows)])
+        for t in range(width // LANES):
+            a, b = t * LANES, (t + 1) * LANES
+            block = gathered[pl.ds(at, rows), a:b]
+            left = split(jnp.where(index < limit, block, 0.0))
+            total[a:b] = total[a:b] + dot3(left, right, ((0,), (0,)))
+
+    def wait_mate(src):
+        for h in range(HALVES):
+            mate_copy(src, h, place(src, h)).wait_recv()
+
+    def multiply_far(s):
+        def one(d, carry):
+            src = z - s + 2 * s * d
+
+            @pl.when((src >= 0) & (src < lines))
+            def _():
+                wait_mate(src)
+                multiply(src)
+
+            return carry
+
+        lax.fori_loop(0, 2, one, 0)
+
+    barrier = pltpu.get_barrier_semaphore()
+    for axis, bit in order:
+        _, other = partner(axis, bit)
+        pl.semaphore_signal(barrier, inc=1, device_id=other, device_id_type=MESH)
+
+    for shift in (1, lines - 1):
+        other = lax.rem(z + shift, lines) * CORES + core
+        pl.semaphore_signal(barrier, inc=1, device_id={"col": other}, device_id_type=MESH)
+    pl.semaphore_wait(barrier, len(order) + 2)
+
+    start_own(0)
+    first = col * rows_dev
+    index = first + lax.broadcasted_iota(jnp.int32, (rows_dev, width), 0)
+    high, low = split(jnp.where(index < limit, panel_ref[...], 0.0))
+    for n, (i, j) in enumerate(blocks_of(width)):
+        a, b = slice(i * LANES, (i + 1) * LANES), slice(j * LANES, (j + 1) * LANES)
+        pack[n * LANES:(n + 1) * LANES] = dot3(
+            (high[:, a], low[:, a]), (high[:, b], low[:, b]), ((0,), (0,))
+        )
+
+    polls = [(s, h) for s in range(1, lines) for h in range(HALVES)]
+    last_z = len(row_bits) + 1
+
+    def after_lines():
+        for h in range(1, HALVES):
+            start_own(h)
+        relay(*polls[0])
+
+    def own_product():
+        total[...] = jnp.zeros_like(total)
+        gathered[pl.ds(pl.multiple_of(first, GROUP), rows_dev)] = panel_ref[...]
+        fetch.wait()
+        wait_mate(z)
+        multiply(z)
+
+    reduce_all(
+        pack, packed, pack_land, send, recv, fold_streams,
+        {("spread", last_z): after_lines, ("spread", last_z - 1): own_product},
+    )
+
     whole[...] = jnp.zeros_like(whole)
     for n, (i, j) in enumerate(blocks_of(width)):
-        whole[i * LANES:(i + 1) * LANES, j * LANES:(j + 1) * LANES] = packed_ref[
+        whole[i * LANES:(i + 1) * LANES, j * LANES:(j + 1) * LANES] = packed[
             n * LANES:(n + 1) * LANES
         ]
     square = lax.broadcasted_iota(jnp.int32, (LANES, LANES), 0)
@@ -198,7 +305,12 @@
         a, b = t * LANES, (t + 1) * LANES
         whole[a:b, width + a:width + b] = unit
 
-    for t in range(width // LANES):
+    waiting = polls[1:]
+    tiles = width // LANES
+    done = 0
+    relay(*waiting[0])
+    passed = 1
+    for t in range(tiles):
         a, b = t * LANES, (t + 1) * LANES
         work[:, :LANES] = whole[a:b, a:b]
         work[:, LANES:] = unit
@@ -216,55 +328,86 @@
             shift = (high[:, LANES:LANES + rest], low[:, LANES:LANES + rest])
             tail = (high[:, LANES:], low[:, LANES:])
             whole[b:, b:width + b] = whole[b:, b:width + b] - dot3(shift, tail, ((0,), (0,)))
+        until = len(waiting) if t == tiles - 1 else 1 + (len(waiting) - 1) * (t + 1) // tiles
+        while passed < until:
+            relay(*waiting[passed])
+            passed += 1
+        complete = (passed + 1) // HALVES if t == tiles - 1 else passed // HALVES
+        while done < complete:
+            done += 1
+            multiply_far(done)
     upper_ref[...] = whole[:, :width]
-    inverse_ref[...] = whole[:, width:]
-
-
-def factorize(packed, width):
-    square = jax.ShapeDtypeStruct((width, width), jnp.float32)
+
+    reduce_all(total, summed, land, send2, recv2, sum_streams)
+    inverse = split(whole[:, width:])
+    out_ref[...] = dot3(inverse, split(summed[...]), ((1,), (0,)))
+
+    for h in range(HALVES):
+        mate_copy(z, h, place(z, h)).wait_send()
+
+        @pl.when(z < lines - 1)
+        def _():
+            send_copy(z, h, place(z, h), right_s, col).wait_send()
+
+        @pl.when(z > 0)
+        def _():
+            send_copy(z, h, place(z, h), left_s, col).wait_send()
+
+    for s, h in polls:
+        @pl.when(z >= s)
+        def _():
+            mate_copy(z - s, h, place(z - s, h)).wait_send()
+
+            @pl.when(z < lines - 1)
+            def _():
+                send_copy(z - s, h, place(z - s, h), right_s, col).wait_send()
+
+        @pl.when(z + s < lines)
+        def _():
+            mate_copy(z + s, h, place(z + s, h)).wait_send()
+
+            @pl.when(z > 0)
+            def _():
+                send_copy(z + s, h, place(z + s, h), left_s, col).wait_send()
+
+
+def body(n_row, n_col, panel, trailing, counts):
+    width = panel.shape[1]
+    rows, columns = bits_of("row", n_row), bits_of("col", n_col)
+    packed_rows = len(blocks_of(width)) * LANES
+    fold = two_streams(packed_rows, rows + columns, rows + columns)
+    total = two_streams(width, rows, rows)
+    chunks = n_col // CORES * HALVES
+    vmem = lambda *shape: pltpu.VMEM(shape, jnp.float32)
+    dma = lambda n: pltpu.SemaphoreType.DMA((n,))
+    spans = trailing.shape[1]
     return pl.pallas_call(
-        factor_kernel,
-        out_shape=(square, square),
-        in_specs=[pl.BlockSpec(memory_space=pltpu.VMEM)],
+        functools.partial(kernel, n_row, n_col),
+        out_shape=(
+            jax.ShapeDtypeStruct((width, width), jnp.float32),
+            jax.ShapeDtypeStruct((width, spans), jnp.float32),
+        ),
+        in_specs=[
+            pl.BlockSpec(memory_space=pltpu.SMEM),
+            pl.BlockSpec(memory_space=pltpu.VMEM),
+            pl.BlockSpec(memory_space=pl.ANY),
+        ],
         out_specs=[pl.BlockSpec(memory_space=pltpu.VMEM)] * 2,
         scratch_shapes=[
-            pltpu.VMEM((width, 2 * width), jnp.float32),
-            pltpu.VMEM((LANES, 2 * LANES), jnp.float32),
+            vmem(packed_rows, LANES), vmem(packed_rows, LANES),
+            vmem(landing_rows(fold), LANES),
+            dma(4 * len(rows + columns)), dma(4 * len(rows + columns)),
+            vmem(*(n_col * panel.shape[0], width)), vmem(*trailing.shape),
+            vmem(width, spans), vmem(width, spans), vmem(landing_rows(total), spans),
+            dma(4 * len(rows)), dma(4 * len(rows)),
+            vmem(width, 2 * width), vmem(LANES, 2 * LANES),
+            pltpu.SemaphoreType.DMA,
+            dma(chunks), dma(chunks), dma(chunks), dma(chunks), dma(chunks),
         ],
-        cost_estimate=pl.CostEstimate(flops=10**9, bytes_accessed=10**8, transcendentals=0),
-    )(packed)
-
-
-def body(n_row, n_col, panel, trailing, counts):
-    width = panel.shape[1]
-    valid = counts[0]
-    piece = lax.all_gather(panel, "col", axis=0, tiled=True)
-
-    own = lax.axis_index("col") * panel.shape[0] + lax.iota(jnp.int32, panel.shape[0])
-    masked = jnp.where((own // width < valid)[:, None], panel, 0.0)
-    rows, columns = bits_of("row", n_row), bits_of("col", n_col)
-    turned = rows[len(rows) // 2:] + rows[:len(rows) // 2]
-    order = columns[:1] + rows + columns[1:]
-    packed_rows = len(blocks_of(width)) * LANES
-    packed = call_reducing(
-        gram_kernel, masked, packed_rows, LANES,
-        two_streams(packed_rows, order, columns[:1] + turned + columns[1:]), order, 0,
-    )
-    upper, inverse = factorize(packed, width)
-
-    indices = lax.iota(jnp.int32, piece.shape[0])
-    piece = jnp.where((indices // width < valid)[:, None], piece, 0.0)
-    cross = lax.dot_general(
-        piece, trailing, (((0,), (0,)), ((), ())),
-        precision=lax.Precision.HIGH, preferred_element_type=jnp.float32,
-    )
-    cross = call_reducing(
-        sum_kernel, cross, width, cross.shape[1], two_streams(width, rows, turned), rows, 1
-    )
-    projected = lax.dot(
-        inverse, cross, precision=lax.Precision.HIGH, preferred_element_type=jnp.float32
-    )
-    return (upper, projected)
+        compiler_params=pltpu.CompilerParams(
+            collective_id=0, has_side_effects=True, vmem_limit_bytes=56 * 2**20
+        ),
+    )(counts, panel, trailing)
 
 
 def solution(mesh):

time: 130 us -> 102 us (0.78)
  matrix products: 14.7 us -> 0 us
  between operations: 14.7 us -> 1.29 us
  local copies, waits for them, and re-layouts: 0.01 us -> 4.52 us
  other arithmetic: 2.16 us -> 0 us
    dot_general x2 -> x0, matrix products: 14.7 us -> none  [the longest x1 11.5 us: body(): lax.dot_general(piece, trailing, (((0,), (0,)), ((), ())), precision=lax....]
    unnamed x2, local copies, waits for them, and re-layouts: 0.01 us -> 4.52 us
    select_n x1 -> x0, other arithmetic: 2.14 us -> none  [body(): masked = jnp.where((own // width < valid)[:, None], panel, 0.0)]
    pallas_call x3 -> x1, Pallas kernels: 97 us -> 96.4 us  [body(): pl.pallas_call(functools.partial(kernel, n_row, n_col), out_shape=(jax.Sh...]
  transfers between devices with their start and end apart: 1 -> 0, of which waited for: 0 -> 0; matrix products, arithmetic and copies ran while one was open for 2% -> 0% of each run, Pallas kernels for 56% -> 0%
where the time goes in v1:
time: 102 us
  Pallas kernels  96.4 us (95%)
  local copies, waits for them, and re-layouts  4.52 us (4%)
  between operations  1.29 us (1%)
    pallas_call x1, Pallas kernels, body(): pl.pallas_call(functools.partial(kernel, n_row, n_col), out_shape=(jax.Sh...  96.4 us
    unnamed x2, local copies, waits for them, and re-layouts  4.52 us

profile of v1, /device:TPU:0, one launch (start us, length us, event | category | flops | bytes accessed | tf_op | source)
XLA Modules:
  0.0 102.2 jit_solution(7694447212056375259)
XLA Ops:
  1.3 96.4 %shard_map.50 = (f32[512,512]{1,0:T(8,128)}, f32[512,512]{1,0:T(8,128)}) custom-call(s32[1]{0:T(128)S(6)} %copy.7.counts_ref, f32[384,512]{1,0:T(8,128)} %panel_ref.1, f32[3072,512]{1,0:T(8,128)} %trailing_hbm.1), custom_call_target="tpu_custom_call" | custom-call | tf_op jit(solution)/shard_map/pallas_call | solution.py:384
  97.7 2.3 %copy.8 = f32[512,512]{1,0:T(8,128)} copy(f32[512,512]{1,0:T(8,128)} %get-tuple-element.4) | data formatting | bytes 2097152
  100.0 2.3 %copy.9 = f32[512,512]{1,0:T(8,128)} copy(f32[512,512]{1,0:T(8,128)} %get-tuple-element.5) | data formatting | bytes 2097152
